TPU v7x, 128 devices: a whole 4x4x4 slice. The times are simulated.
128 devices in a mesh: blk: 64 (over x, z, y_lo, core), ep: 2 (over y_hi).
Axes of the slice: x: 4, y: 4 (y_hi: 2, y_lo: 2; y = y_hi * 2 + y_lo), z: 4, core: 2. Of those that a mesh axis runs over, the one named last changes fastest.
Arguments:
- hidden_in: bfloat16 [1024, 4096], P('blk'), may hold values from -6 to 6
- out_grad: bfloat16 [1024, 4096], P('blk'), may hold values from -6 to 6
- expert_ids: int32 [1024, 2], P('blk'), may hold values from 0 to 3, all different within a row; in each aligned block of 16 rows (0 to 15, 16 to 31, ...) at most 12 rows name the same one
- gate_values: bfloat16 [1024, 2], P('blk'), may hold values from 0.099609375 to 1
- w_gate: bfloat16 [4, 14336, 4096], P('ep', 'blk'), may hold values from -0.09375 to 0.09375
- w_up: bfloat16 [4, 14336, 4096], P('ep', 'blk'), may hold values from -0.09375 to 0.09375
- w_down: bfloat16 [4, 14336, 4096], P('ep', 'blk'), may hold values from -0.046875 to 0.046875
Outputs:
- input_grad: bfloat16 [1024, 4096], P('blk')
- gate_grad: float32 [1024, 2], P('blk')
- grad_gate: bfloat16 [4, 14336, 4096], P('ep', 'blk')
- grad_up: bfloat16 [4, 14336, 4096], P('ep', 'blk')
- grad_down: bfloat16 [4, 14336, 4096], P('ep', 'blk')
Inputs may be any that keep to these rules, and one draw needn't show every extreme that they name: `expert_ids`: each row names 2 different experts; in each aligned block of 16 rows (the rows of one device) no expert is named by more than 12 rows, a bound that some block reaches.
All inputs are finite; a program needn't handle non-finite values.
Results may differ from a plain program's by a relative error of at most 0.008.
Values may be sent and summed in bfloat16 or wider, within the bound.
No kernel may reach another device: no remote copies, remote signals or barrier semaphores. Data moves between devices by JAX's collectives and lax.ppermute only.
A program may use at most 256 MiB of HBM per device.

v0:
```python
import jax
import jax.numpy as jnp
from jax import lax
from jax.sharding import PartitionSpec as P

TOK_DEV = 16
CAP = 12


def sent_together(arrays, axis, dim, along):
    ends, at = ([], 0)
    for a in arrays[:-1]:
        at += a.shape[along]
        ends.append(at)
    both = jnp.concatenate(arrays, axis=along)
    return tuple(jnp.split(lax.all_gather(both, axis, axis=dim, tiled=True), ends, axis=along))


def side_by_side(arrays, axis, dim, along):
    both = jnp.concatenate(arrays, axis=along)
    filled, at, gathered = (lax.psum_scatter(both, axis, scatter_dimension=dim, tiled=True), 0, [])
    for a in arrays:
        gathered.append(lax.slice_in_dim(filled, at, at + a.shape[along], axis=along))
        at += a.shape[along]
    return tuple(gathered)


def sent_to_all(value, axis):
    copies = jnp.broadcast_to(value, (lax.axis_size(axis), *value.shape))
    return lax.all_to_all(copies, axis, split_axis=0, concat_axis=0, tiled=True)


def taken_together(value, axis):
    return sent_to_all(value, axis).astype(jnp.float32).sum(axis=0)


def routed(expert_ids, gate_values, expert, blocks):
    chosen = expert_ids == expert
    hits = jnp.any(chosen, axis=1).astype(jnp.int32).reshape(blocks, TOK_DEV)
    weight = jnp.sum(
        jnp.where(chosen, gate_values.astype(jnp.float32), jnp.float32(0.0)), axis=1
    ).reshape(blocks, TOK_DEV)
    position = jnp.cumsum(hits, axis=1) - hits
    slot_index = lax.broadcasted_iota(jnp.int32, (blocks, CAP, TOK_DEV), 1)
    picked = (position[:, None, :] == slot_index) & (hits[:, None, :] > 0)
    selector = jnp.where(picked, jnp.float32(1.0), jnp.float32(0.0))
    return (selector, weight, chosen)


def expert_pass(selector, weight, hidden_in, out_grad, gate_mat, up_mat, down_mat, blocks):
    width = hidden_in.shape[1]
    select_low = selector.astype(jnp.bfloat16)
    x_slots = (
        jnp.einsum(
            "bct,btd->bcd",
            select_low,
            hidden_in.reshape(blocks, TOK_DEV, width),
            preferred_element_type=jnp.float32,
        )
        .astype(jnp.bfloat16)
        .reshape(-1, width)
    )
    dy_slots = (
        jnp.einsum(
            "bct,btd->bcd",
            select_low,
            out_grad.reshape(blocks, TOK_DEV, width),
            preferred_element_type=jnp.float32,
        )
        .astype(jnp.bfloat16)
        .reshape(-1, width)
    )
    slot_weight = jnp.einsum("bct,bt->bc", selector, weight).reshape(-1, 1)
    contract_cols = (((1,), (1,)), ((), ()))
    gate_pre = lax.dot_general(x_slots, gate_mat, contract_cols, preferred_element_type=jnp.float32)
    up_pre = lax.dot_general(x_slots, up_mat, contract_cols, preferred_element_type=jnp.float32)
    back = lax.dot_general(dy_slots, down_mat, contract_cols, preferred_element_type=jnp.float32)
    sigmoid_gate = jax.nn.sigmoid(gate_pre)
    activation = gate_pre * sigmoid_gate * up_pre
    slot_gate = jnp.sum(activation * back, axis=1)
    dact = slot_weight * back
    d_up = (dact * gate_pre * sigmoid_gate).astype(jnp.bfloat16)
    d_gate = (dact * up_pre * sigmoid_gate * (1.0 + gate_pre * (1.0 - sigmoid_gate))).astype(
        jnp.bfloat16
    )
    act_low = activation.astype(jnp.bfloat16)
    dy_weighted = (slot_weight * dy_slots.astype(jnp.float32)).astype(jnp.bfloat16)
    contract_rows = (((0,), (0,)), ((), ()))
    grad_g = lax.dot_general(
        d_gate, x_slots, contract_rows, preferred_element_type=jnp.float32
    ).astype(jnp.bfloat16)
    grad_u = lax.dot_general(
        d_up, x_slots, contract_rows, preferred_element_type=jnp.float32
    ).astype(jnp.bfloat16)
    grad_d = lax.dot_general(
        act_low, dy_weighted, contract_rows, preferred_element_type=jnp.float32
    ).astype(jnp.bfloat16)
    dx_slots = jnp.dot(d_gate, gate_mat, preferred_element_type=jnp.float32) + jnp.dot(
        d_up, up_mat, preferred_element_type=jnp.float32
    )
    dx_tokens = jnp.einsum("bct,bcd->btd", selector, dx_slots.reshape(blocks, CAP, width)).reshape(
        -1, width
    )
    gate_tokens = jnp.einsum("bct,bc->bt", selector, slot_gate.reshape(blocks, CAP)).reshape(-1)
    return (grad_g, grad_u, grad_d, dx_tokens, gate_tokens)


def shards(hidden_in, out_grad, expert_ids, gate_values, w_gate, w_up, w_down):
    whole_x, whole_dy, whole_ids, whole_gates = (
        *sent_together((hidden_in, out_grad), "blk", 0, 1),
        lax.all_gather(expert_ids, "blk", axis=0, tiled=True),
        lax.all_gather(gate_values, "blk", axis=0, tiled=True),
    )
    blocks = whole_x.shape[0] // TOK_DEV
    first_expert = lax.axis_index("ep") * w_gate.shape[0]
    token_grad = jnp.zeros(whole_x.shape, jnp.float32)
    gate_grad = jnp.zeros(whole_ids.shape, jnp.float32)
    grads_g, grads_u, grads_d = ([], [], [])
    for local_expert in range(w_gate.shape[0]):
        selector, weight, chosen = routed(
            whole_ids, whole_gates, first_expert + local_expert, blocks
        )
        grad_g, grad_u, grad_d, dx_tokens, gate_tokens = expert_pass(
            selector,
            weight,
            whole_x,
            whole_dy,
            w_gate[local_expert],
            w_up[local_expert],
            w_down[local_expert],
            blocks,
        )
        grads_g.append(grad_g)
        grads_u.append(grad_u)
        grads_d.append(grad_d)
        token_grad = token_grad + dx_tokens
        gate_grad = gate_grad + jnp.where(chosen, gate_tokens[:, None], jnp.float32(0.0))
    part_x, part_g = side_by_side((token_grad, gate_grad), "blk", 0, 1)
    summed_x, gate_out = (
        taken_together(part_x.astype(jnp.bfloat16), "ep").astype(jnp.float32),
        taken_together(part_g.astype(jnp.bfloat16), "ep").astype(jnp.float32),
    )
    input_grad = summed_x.astype(jnp.bfloat16)
    return (input_grad, gate_out, jnp.stack(grads_g), jnp.stack(grads_u), jnp.stack(grads_d))


def solution(mesh):
    in_specs = (
        P("blk", None),
        P("blk", None),
        P("blk", None),
        P("blk", None),
        P("ep", "blk", None),
        P("ep", "blk", None),
        P("ep", "blk", None),
    )
    out_specs = (
        P("blk", None),
        P("blk", None),
        P("ep", "blk", None),
        P("ep", "blk", None),
        P("ep", "blk", None),
    )
    return jax.shard_map(shards, mesh=mesh, in_specs=in_specs, out_specs=out_specs, check_vma=False)
```

profile of v0, /device:TPU:0, one launch (start us, length us, event | category | flops | bytes accessed | tf_op | source)
XLA Modules:
  0.0 689.4 jit_solution(14464461744498951361)
XLA Ops:
  9.0 83.9 %all-gather = s32[64,16,2]{1,2,0:T(2,128)S(1)} all-gather(s32[1,16,2]{1,2,0:T(2,128)} %bitcast.126), channel_id=1, replica_groups=mesh['blk'=64,'ep'=2] {'blk'}, dimensions={0}, use_global_device_ids=true | all-gather | bytes 8320 | tf_op jit(solution)/shard_map/all_gather | solution.py:111
  95.2 76.7 %all-gather.1 = bf16[64,16,2]{1,2,0:T(2,128)(2,1)S(1)} all-gather(bf16[1,16,2]{1,2,0:T(2,128)(2,1)} %bitcast.127), channel_id=1, replica_groups=mesh['blk'=64,'ep'=2] {'blk'}, dimensions={0}, use_global_device_ids=true | all-gather | bytes 4160 | tf_op jit(solution)/shard_map/all_gather | solution.py:112
  173.8 6.7 fusion.50
  180.5 5.6 convolution_convert_fusion.2
  186.0 5.6 convolution_convert_fusion.3
  191.6 5.6 convolution_convert_fusion
  197.2 5.6 convolution_convert_fusion.1
  202.7 10.0 %reshape.115 = bf16[768,4096]{1,0:T(8,128)(2,1)} reshape(bf16[64,12,4096]{2,1,0:T(8,128)(2,1)} %convolution_convert_fusion.2) | data formatting | bytes 12582912 | tf_op jit(solution)/shard_map/reshape | solution.py:61
  212.7 9.9 %reshape.113 = bf16[768,4096]{1,0:T(8,128)(2,1)} reshape(bf16[64,12,4096]{2,1,0:T(8,128)(2,1)} %convolution_convert_fusion.3) | data formatting | bytes 12582912 | tf_op jit(solution)/shard_map/reshape | solution.py:71
  222.6 10.1 %reshape.119 = bf16[768,4096]{1,0:T(8,128)(2,1)} reshape(bf16[64,12,4096]{2,1,0:T(8,128)(2,1)} %convolution_convert_fusion) | data formatting | bytes 12582912 | tf_op jit(solution)/shard_map/reshape | solution.py:61
  232.7 5.5 fusion.26
  238.9 2.9 fusion.17
  241.8 9.9 %reshape.118 = bf16[768,4096]{1,0:T(8,128)(2,1)} reshape(bf16[64,12,4096]{2,1,0:T(8,128)(2,1)} %convolution_convert_fusion.1) | data formatting | bytes 12582912 | tf_op jit(solution)/shard_map/reshape | solution.py:71
  251.7 5.5 fusion.28
  257.3 4.5 fusion.19
  261.8 3.2 multiply_convert_fusion.15
  267.1 4.6 convolution_add_fusion.2
  271.7 10.2 %reshape.116 = bf16[64,12,4096]{2,1,0:T(8,128)(2,1)} reshape(bf16[768,4096]{1,0:T(8,128)(2,1)} %convolution_add_fusion.2) | data formatting | bytes 12582912 | tf_op jit(solution)/shard_map/reshape | solution.py:101
  281.9 6.9 %multiply_convert_fusion.13 = (bf16[768,224]{0,1:T(8,128)(2,1)S(1)}, f32[768]{0:T(1024)S(1)}, bf16[768,224]{0,1:T(8,128)(2,1)S(1)}, f32[768,224]{0,1:T(8,128)}) fusion(f32[768,224]{0,1:T(8,128)} %fusion.17, f32[768,224]{0,1:T(8,128)} %fusion.19, f32[768]{0:T(1024)S(1)} %mul.103, bf16[768,4096]{1,0:T(8,128)(2,1)} %reshape.119, bf16[2,224,4096]{2,1,0:T(8,128)(2,1)} %param.11), kind=kOutput, calls=%fused_computation.62 | convolution fusion | flops 1412381952 | bytes 10885120 | tf_op jit(solution)/shard_map/dot_general | solution.py:75
  290.8 4.5 convolution_add_fusion.1
  295.4 9.8 %reshape.120 = bf16[64,12,4096]{2,1,0:T(8,128)(2,1)} reshape(bf16[768,4096]{1,0:T(8,128)(2,1)} %convolution_add_fusion.1) | data formatting | bytes 12582912 | tf_op jit(solution)/shard_map/reshape | solution.py:101
  306.2 11.5 %fusion.52 = f32[64,16,4096]{2,1,0:T(8,128)} fusion(bf16[64,12,16]{1,2,0:T(8,128)(2,1)S(1)} %copy.49, bf16[64,12,4096]{2,1,0:T(8,128)(2,1)} %reshape.116), kind=kOutput, calls=%fused_computation.92 | convolution fusion | flops 100663296 | bytes 23093248 | tf_op jit(solution)/shard_map/bct,bcd->btd/dot_general | solution.py:101
  317.7 16.2 %convolution_add_fusion = f32[64,16,4096]{2,1,0:T(8,128)} fusion(f32[64,16,4096]{2,1,0:T(8,128)} %fusion.52, bf16[64,12,16]{1,2,0:T(8,128)(2,1)S(1)} %copy.55, bf16[64,12,4096]{2,1,0:T(8,128)(2,1)} %reshape.120), kind=kOutput, calls=%fused_computation.3 | convolution fusion | flops 104857600 | bytes 39870464 | tf_op jit(solution)/shard_map/bct,bcd->btd/dot_general | solution.py:101
  333.9 11.6 %pad_maximum_fusion = f32[1024,4098]{1,0:T(8,128)} fusion(f32[1024,2]{1,0:T(8,128)S(1)} %copy.56, f32[1024,4096]{1,0:T(8,128)} %bitcast.107), kind=kLoop, calls=%fused_computation | loop fusion | flops 4196352 | bytes 33570816 | tf_op jit(solution)/shard_map/concatenate | solution.py:20
  345.6 4.5 fusion.8
  350.2 4.6 fusion.9
  357.7 2.9 fusion.7
  368.8 290.9 %reduce-scatter.2.cloned.1.call-done = f32[16,4098]{1,0:T(8,128)} async-done(((f32[1024,4098]{1,0:T(8,128)}), f32[16,4098]{1,0:T(8,128)}) %reduce-scatter.2.cloned.1.call-update) | async-done | bytes 262288 | tf_op jit(solution)/shard_map/reduce_scatter | solution.py:21
  661.4 4.2 all-to-all-start.1
  665.6 5.2 all-to-all-done.1
  671.5 3.4 all-to-all-start
  675.0 3.7 pad_maximum_fusion.1
  (115 shorter events, 28.6 us)
Async XLA Ops:
  7.2 166.6 %all-gather.4.cloned.1.call-start = ((), (), s32[]{:S(2)}) async-start(), calls=%async_computation.3 | async-start | bytes 17039360 | tf_op jit(solution)/shard_map/all_gather | solution.py:16
  8.9 650.8 %reduce-scatter.2.cloned.1.call-start = ((), (), s32[]{:S(2)}) async-start(), calls=%async_computation.4 | async-start | bytes 17571840 | tf_op jit(solution)/shard_map/reduce_scatter | solution.py:21
  232.7 5.5 copy-start.1
  232.7 6.2 copy-start.2
  238.9 22.9 %copy-start.9 = (f32[768,224]{0,1:T(8,128)}, f32[768,224]{0,1:T(8,128)S(1)}, u32[]{:S(2)}) copy-start(f32[768,224]{0,1:T(8,128)S(1)} %fusion.26) | copy-start | bytes 2064388
  251.7 5.5 copy-start
  251.7 10.1 %slice-start.4 = ((s8[6291456]{0:T(1024)(128)(4,1)}), s8[4194304]{0:T(1024)(128)(4,1)S(1)}, s32[]{:S(2)}) async-start(s8[6291456]{0:T(1024)(128)(4,1)} %bitcast.112), calls=%async_computation.9 | async-start | bytes 8388608
  257.2 4.6 slice-start.5
  257.3 4.6 copy-start.5
  265.1 2.0 copy-start.3
  281.9 6.9 %copy-start.6 = (bf16[2,224,4096]{2,1,0:T(8,128)(2,1)S(1)}, bf16[2,224,4096]{2,1,0:T(8,128)(2,1)}, u32[]{:S(2)}) copy-start(bf16[2,224,4096]{2,1,0:T(8,128)(2,1)} %param.11) | copy-start | bytes 11010052
  288.8 2.0 copy-start.4
  345.6 9.2 %slice-start.6 = ((s8[6291456]{0:T(1024)(128)(4,1)}), s8[2097152]{0:T(1024)(128)(4,1)S(1)}, s32[]{:S(2)}) async-start(s8[6291456]{0:T(1024)(128)(4,1)} %bitcast.114), calls=%async_computation.11 | async-start | bytes 4194304
  345.6 9.2 %slice-start.7 = ((s8[6291456]{0:T(1024)(128)(4,1)}), s8[4194304]{0:T(1024)(128)(4,1)S(1)}, s32[]{:S(2)}) async-start(s8[6291456]{0:T(1024)(128)(4,1)} %bitcast.114), calls=%async_computation.12 | async-start | bytes 8388608
  350.2 7.5 %slice-start.8 = ((s8[6291456]{0:T(1024)(128)(4,1)}), s8[4194304]{0:T(1024)(128)(4,1)S(1)}, s32[]{:S(2)}) async-start(s8[6291456]{0:T(1024)(128)(4,1)} %bitcast.116), calls=%async_computation.13 | async-start | bytes 8388608
  350.2 10.4 %slice-start.2 = ((s8[6291456]{0:T(1024)(128)(4,1)}), s8[4194304]{0:T(1024)(128)(4,1)S(1)}, s32[]{:S(2)}) async-start(s8[6291456]{0:T(1024)(128)(4,1)} %bitcast.110), calls=%async_computation.7 | async-start | bytes 8388608
  354.8 2.9 slice-start.9
  354.8 5.8 slice-start.3
  357.7 3.0 copy-start.10
  357.7 3.0 copy-start.11
  357.7 4.9 slice-start
  360.6 1.9 slice-start.1
  360.6 1.9 copy-start.8
  360.7 2.0 copy-start.12
  366.7 308.3 %copy-start.7 = (bf16[1,224,4096]{2,1,0:T(8,128)(2,1)S(1)}, bf16[1,224,4096]{2,1,0:T(8,128)(2,1)}, u32[]{:S(2)}) copy-start(bf16[1,224,4096]{2,1,0:T(8,128)(2,1)} %fusion.6) | copy-start | bytes 5505028
  661.4 9.4 %all-to-all-start.1 = ((bf16[2,16,2]{1,2,0:T(2,128)(2,1)}), bf16[2,16,2]{1,2,0:T(2,128)(2,1)S(1)}, u32[]{:S(2)}, u32[]{:S(2)}) async-start(bf16[2,16,2]{1,2,0:T(2,128)(2,1)} %broadcast_in_dim.51), calls=%async_computation.2 | async-start | bytes 2048 | tf_op jit(solution)/shard_map/all_to_all | solution.py:30
  671.5 10.1 %all-to-all-start = ((bf16[2,16,4096]{2,1,0:T(8,128)(2,1)}), bf16[2,16,4096]{2,1,0:T(8,128)(2,1)S(1)}, u32[]{:S(2)}, u32[]{:S(2)}) async-start(bf16[2,16,4096]{2,1,0:T(8,128)(2,1)} %broadcast_in_dim.50), calls=%async_computation.1 | async-start | bytes 524288 | tf_op jit(solution)/shard_map/all_to_all | solution.py:30
Sparse Core Ops, SparseCore 0:
  10.3 124.1 all-gather.3
  345.7 313.9 reduce-scatter.1
where the time goes:
time: 695 us; the launch traced here: 689 us
  waiting for transfers between devices  299 us (43%)
  blocking collectives  161 us (23%)
  matrix products  111 us (16%)
  local copies, waits for them, and re-layouts  72.4 us (10%)
  other arithmetic  24.3 us (3%)
  between operations  14.8 us (2%)
  starting transfers between devices  7.72 us (1%)
    reduce_scatter x1, waiting for transfers between devices, side_by_side(): lax.psum_scatter(both, axis, scatter_dimension=dim, tiled=True)  291 us
    all_gather x1, blocking collectives, shards(): lax.all_gather(expert_ids, 'blk', axis=0, tiled=True)  83.9 us
    all_gather x1, blocking collectives, shards(): lax.all_gather(gate_values, 'blk', axis=0, tiled=True)  76.7 us
    dot_general x2, matrix products, expert_pass(): jnp.einsum('bct,bcd->btd', selector, dx_slots.reshape(blocks, CAP, width))  27.8 us
    reshape x2, local copies, waits for them, and re-layouts, expert_pass(): x_slots = jnp.einsum('bct,btd->bcd', select_low, hidden_in.reshape(blocks...  20.1 us
    reshape x2, local copies, waits for them, and re-layouts, expert_pass(): dx_slots.reshape(blocks, CAP, width)  19.9 us
    reshape x2, local copies, waits for them, and re-layouts, expert_pass(): dy_slots = jnp.einsum('bct,btd->bcd', select_low, out_grad.reshape(blocks...  19.8 us
  transfers between devices with their start and end apart: 4, of which 3 were waited for; matrix products, arithmetic and copies ran while one was open for 5% of the time, Pallas kernels for 0%

commit v1 on v0

--- a/solution.py
+++ b/solution.py
@@ -108,7 +108,9 @@
 def shards(hidden_in, out_grad, expert_ids, gate_values, w_gate, w_up, w_down):
     whole_x, whole_dy, whole_ids, whole_gates = (
         *sent_together((hidden_in, out_grad), "blk", 0, 1),
-        lax.all_gather(expert_ids, "blk", axis=0, tiled=True),
+        jnp.concatenate(
+            lax.all_to_all(jnp.stack([expert_ids] * lax.axis_size("blk")), "blk", 0, 0), axis=0
+        ),
         lax.all_gather(gate_values, "blk", axis=0, tiled=True),
     )
     blocks = whole_x.shape[0] // TOK_DEV

time: 695 us -> 658 us (0.947)
  blocking collectives: 161 us -> 82.5 us
  waiting for transfers between devices: 299 us -> 328 us
  starting transfers between devices: 7.72 us -> 17.6 us
    all_gather x1 -> x0, blocking collectives: 83.9 us -> none  [shards(): lax.all_gather(expert_ids, 'blk', axis=0, tiled=True)]
    all_gather x1, waiting for transfers between devices: 0.02 us -> 27.6 us  [sent_together(): lax.all_gather(both, axis, axis=dim, tiled=True)]
    all_to_all x0 -> x1, starting transfers between devices: none -> 9.91 us  [shards(): lax.all_to_all(jnp.stack([expert_ids] * lax.axis_size('blk')), 'blk', 0, 0)]
  transfers between devices with their start and end apart: 4 -> 5, of which waited for: 3 -> 4; matrix products, arithmetic and copies ran while one was open for 5% -> 5% of each run, Pallas kernels for 0% -> 0%
where the time goes in v1:
time: 658 us; the launch traced here: 652 us
  waiting for transfers between devices  328 us (50%)
  matrix products  111 us (17%)
  blocking collectives  82.5 us (13%)
  local copies, waits for them, and re-layouts  73.8 us (11%)
  other arithmetic  24.3 us (4%)
  starting transfers between devices  17.6 us (3%)
  between operations  14.8 us (2%)
    reduce_scatter x1, waiting for transfers between devices, side_by_side(): lax.psum_scatter(both, axis, scatter_dimension=dim, tiled=True)  293 us
    all_gather x1, blocking collectives, shards(): lax.all_gather(gate_values, 'blk', axis=0, tiled=True)  82.5 us
    dot_general x2, matrix products, expert_pass(): jnp.einsum('bct,bcd->btd', selector, dx_slots.reshape(blocks, CAP, width))  27.8 us
    all_gather x1, waiting for transfers between devices, sent_together(): lax.all_gather(both, axis, axis=dim, tiled=True)  27.6 us
    reshape x2, local copies, waits for them, and re-layouts, expert_pass(): x_slots = jnp.einsum('bct,btd->bcd', select_low, hidden_in.reshape(blocks...  20.1 us
    reshape x2, local copies, waits for them, and re-layouts, expert_pass(): dx_slots.reshape(blocks, CAP, width)  19.9 us
    reshape x2, local copies, waits for them, and re-layouts, expert_pass(): dy_slots = jnp.einsum('bct,btd->bcd', select_low, out_grad.reshape(blocks...  19.8 us
  transfers between devices with their start and end apart: 5, of which 4 were waited for; matrix products, arithmetic and copies ran while one was open for 5% of the time, Pallas kernels for 0%

profile of v1, /device:TPU:0, one launch (start us, length us, event | category | flops | bytes accessed | tf_op | source)
XLA Modules:
  0.0 652.3 jit_solution(10306818015284191074)
XLA Ops:
  10.3 9.9 %all-to-all-start = ((s32[64,16,2]{1,2,0:T(2,128)}), s32[64,16,2]{1,2,0:T(2,128)S(1)}, u32[]{:S(2)}, u32[]{:S(2)}) async-start(s32[64,16,2]{1,2,0:T(2,128)} %stack.20), calls=%async_computation | async-start | bytes 131072 | tf_op jit(solution)/shard_map/all_to_all | solution.py:112
  20.2 82.5 %all-gather = bf16[64,16,2]{1,2,0:T(2,128)(2,1)S(1)} all-gather(bf16[1,16,2]{1,2,0:T(2,128)(2,1)} %bitcast.125), channel_id=1, replica_groups=mesh['blk'=64,'ep'=2] {'blk'}, dimensions={0}, use_global_device_ids=true | all-gather | bytes 4160 | tf_op jit(solution)/shard_map/all_gather | solution.py:114
  106.9 27.6 %all-gather.3.cloned.1.call-done = bf16[1024,8192]{1,0:T(8,128)(2,1)} async-done(((bf16[16,8192]{1,0:T(8,128)(2,1)}), bf16[1024,8192]{1,0:T(8,128)(2,1)}) %all-gather.3.cloned.1.call-update) | async-done | bytes 16777232 | tf_op jit(solution)/shard_map/all_gather | solution.py:16
  134.5 6.7 %fusion.50 = (bf16[1024,4096]{1,0:T(8,128)(2,1)S(1)}, bf16[1024,4096]{1,0:T(8,128)(2,1)S(1)}) fusion(bf16[1024,8192]{1,0:T(8,128)(2,1)} %all-gather.3.cloned.1.call-done), kind=kLoop, calls=%fused_computation.90 | loop fusion | bytes 33554432 | tf_op jit(solution)/shard_map/split | solution.py:16
  141.2 5.6 convolution_convert_fusion.2
  146.8 5.6 convolution_convert_fusion.3
  152.3 5.6 convolution_convert_fusion
  157.9 5.6 convolution_convert_fusion.1
  163.4 10.0 %reshape.116 = bf16[768,4096]{1,0:T(8,128)(2,1)} reshape(bf16[64,12,4096]{2,1,0:T(8,128)(2,1)} %convolution_convert_fusion.2) | data formatting | bytes 12582912 | tf_op jit(solution)/shard_map/reshape | solution.py:61
  173.4 9.9 %reshape.114 = bf16[768,4096]{1,0:T(8,128)(2,1)} reshape(bf16[64,12,4096]{2,1,0:T(8,128)(2,1)} %convolution_convert_fusion.3) | data formatting | bytes 12582912 | tf_op jit(solution)/shard_map/reshape | solution.py:71
  183.3 10.1 %reshape.120 = bf16[768,4096]{1,0:T(8,128)(2,1)} reshape(bf16[64,12,4096]{2,1,0:T(8,128)(2,1)} %convolution_convert_fusion) | data formatting | bytes 12582912 | tf_op jit(solution)/shard_map/reshape | solution.py:61
  193.4 5.5 fusion.26
  202.5 9.9 %reshape.119 = bf16[768,4096]{1,0:T(8,128)(2,1)} reshape(bf16[64,12,4096]{2,1,0:T(8,128)(2,1)} %convolution_convert_fusion.1) | data formatting | bytes 12582912 | tf_op jit(solution)/shard_map/reshape | solution.py:71
  212.4 5.5 fusion.28
  218.0 4.5 fusion.19
  222.6 3.2 multiply_convert_fusion.15
  227.8 4.6 convolution_add_fusion.2
  232.4 10.2 %reshape.117 = bf16[64,12,4096]{2,1,0:T(8,128)(2,1)} reshape(bf16[768,4096]{1,0:T(8,128)(2,1)} %convolution_add_fusion.2) | data formatting | bytes 12582912 | tf_op jit(solution)/shard_map/reshape | solution.py:101
  242.6 6.9 %multiply_convert_fusion.13 = (bf16[768,224]{0,1:T(8,128)(2,1)S(1)}, f32[768]{0:T(1024)S(1)}, bf16[768,224]{0,1:T(8,128)(2,1)S(1)}, f32[768,224]{0,1:T(8,128)}) fusion(f32[768,224]{0,1:T(8,128)} %fusion.17, f32[768,224]{0,1:T(8,128)} %fusion.19, f32[768]{0:T(1024)S(1)} %mul.103, bf16[768,4096]{1,0:T(8,128)(2,1)} %reshape.120, bf16[2,224,4096]{2,1,0:T(8,128)(2,1)} %param.11), kind=kOutput, calls=%fused_computation.62 | convolution fusion | flops 1412381952 | bytes 10885120 | tf_op jit(solution)/shard_map/dot_general | solution.py:75
  251.6 4.5 convolution_add_fusion.1
  256.1 9.8 %reshape.121 = bf16[64,12,4096]{2,1,0:T(8,128)(2,1)} reshape(bf16[768,4096]{1,0:T(8,128)(2,1)} %convolution_add_fusion.1) | data formatting | bytes 12582912 | tf_op jit(solution)/shard_map/reshape | solution.py:101
  266.9 11.5 %fusion.52 = f32[64,16,4096]{2,1,0:T(8,128)} fusion(bf16[64,12,16]{1,2,0:T(8,128)(2,1)S(1)} %copy.54, bf16[64,12,4096]{2,1,0:T(8,128)(2,1)} %reshape.117), kind=kOutput, calls=%fused_computation.92 | convolution fusion | flops 100663296 | bytes 23093248 | tf_op jit(solution)/shard_map/bct,bcd->btd/dot_general | solution.py:101
  278.4 16.2 %convolution_add_fusion = f32[64,16,4096]{2,1,0:T(8,128)} fusion(f32[64,16,4096]{2,1,0:T(8,128)} %fusion.52, bf16[64,12,16]{1,2,0:T(8,128)(2,1)S(1)} %copy.60, bf16[64,12,4096]{2,1,0:T(8,128)(2,1)} %reshape.121), kind=kOutput, calls=%fused_computation.3 | convolution fusion | flops 104857600 | bytes 39870464 | tf_op jit(solution)/shard_map/bct,bcd->btd/dot_general | solution.py:101
  294.7 11.6 %pad_maximum_fusion = f32[1024,4098]{1,0:T(8,128)} fusion(f32[1024,2]{1,0:T(8,128)S(1)} %copy.61, f32[1024,4096]{1,0:T(8,128)} %bitcast.106), kind=kLoop, calls=%fused_computation | loop fusion | flops 4196352 | bytes 33570816 | tf_op jit(solution)/shard_map/concatenate | solution.py:20
  306.3 4.5 fusion.8
  310.9 4.5 fusion.9
  318.3 2.9 fusion.7
  329.5 293.2 %reduce-scatter.2.cloned.1.call-done = f32[16,4098]{1,0:T(8,128)} async-done(((f32[1024,4098]{1,0:T(8,128)}), f32[16,4098]{1,0:T(8,128)}) %reduce-scatter.2.cloned.1.call-update) | async-done | bytes 262288 | tf_op jit(solution)/shard_map/reduce_scatter | solution.py:21
  624.3 4.2 all-to-all-start.2
  628.5 5.2 all-to-all-done.2
  634.4 3.4 all-to-all-start.1
  637.9 3.7 pad_maximum_fusion.1
  (117 shorter events, 32.9 us)
Async XLA Ops:
  7.2 127.3 %all-gather.3.cloned.1.call-start = ((), (), s32[]{:S(2)}) async-start(), calls=%async_computation.4 | async-start | bytes 17039360 | tf_op jit(solution)/shard_map/all_gather | solution.py:16
  10.3 92.7 %all-to-all-start = ((s32[64,16,2]{1,2,0:T(2,128)}), s32[64,16,2]{1,2,0:T(2,128)S(1)}, u32[]{:S(2)}, u32[]{:S(2)}) async-start(s32[64,16,2]{1,2,0:T(2,128)} %stack.20), calls=%async_computation | async-start | bytes 131072 | tf_op jit(solution)/shard_map/all_to_all | solution.py:112
  20.2 602.5 %reduce-scatter.2.cloned.1.call-start = ((), (), s32[]{:S(2)}) async-start(), calls=%async_computation.5 | async-start | bytes 17571840 | tf_op jit(solution)/shard_map/reduce_scatter | solution.py:21
  193.4 5.5 copy-start.1
  193.4 6.2 copy-start.2
  199.6 22.9 %copy-start.9 = (f32[768,224]{0,1:T(8,128)}, f32[768,224]{0,1:T(8,128)S(1)}, u32[]{:S(2)}) copy-start(f32[768,224]{0,1:T(8,128)S(1)} %fusion.26) | copy-start | bytes 2064388
  212.4 5.5 copy-start
  212.4 10.1 %slice-start.4 = ((s8[6291456]{0:T(1024)(128)(4,1)}), s8[4194304]{0:T(1024)(128)(4,1)S(1)}, s32[]{:S(2)}) async-start(s8[6291456]{0:T(1024)(128)(4,1)} %bitcast.111), calls=%async_computation.10 | async-start | bytes 8388608
  218.0 4.6 slice-start.5
  218.0 4.6 copy-start.5
  225.8 2.0 copy-start.3
  242.6 6.9 %copy-start.6 = (bf16[2,224,4096]{2,1,0:T(8,128)(2,1)S(1)}, bf16[2,224,4096]{2,1,0:T(8,128)(2,1)}, u32[]{:S(2)}) copy-start(bf16[2,224,4096]{2,1,0:T(8,128)(2,1)} %param.11) | copy-start | bytes 11010052
  249.5 2.0 copy-start.4
  306.3 9.1 %slice-start.6 = ((s8[6291456]{0:T(1024)(128)(4,1)}), s8[2097152]{0:T(1024)(128)(4,1)S(1)}, s32[]{:S(2)}) async-start(s8[6291456]{0:T(1024)(128)(4,1)} %bitcast.113), calls=%async_computation.12 | async-start | bytes 4194304
  306.3 9.1 %slice-start.7 = ((s8[6291456]{0:T(1024)(128)(4,1)}), s8[4194304]{0:T(1024)(128)(4,1)S(1)}, s32[]{:S(2)}) async-start(s8[6291456]{0:T(1024)(128)(4,1)} %bitcast.113), calls=%async_computation.13 | async-start | bytes 8388608
  310.9 7.4 %slice-start.8 = ((s8[6291456]{0:T(1024)(128)(4,1)}), s8[4194304]{0:T(1024)(128)(4,1)S(1)}, s32[]{:S(2)}) async-start(s8[6291456]{0:T(1024)(128)(4,1)} %bitcast.115), calls=%async_computation.14 | async-start | bytes 8388608
  310.9 10.4 %slice-start.2 = ((s8[6291456]{0:T(1024)(128)(4,1)}), s8[4194304]{0:T(1024)(128)(4,1)S(1)}, s32[]{:S(2)}) async-start(s8[6291456]{0:T(1024)(128)(4,1)} %bitcast.109), calls=%async_computation.8 | async-start | bytes 8388608
  315.5 2.9 slice-start.9
  315.5 5.8 slice-start.3
  318.3 3.0 copy-start.10
  318.3 3.0 copy-start.11
  318.3 4.9 slice-start
  321.3 1.9 slice-start.1
  321.3 1.9 copy-start.8
  321.3 2.0 copy-start.12
  327.3 310.5 %copy-start.7 = (bf16[1,224,4096]{2,1,0:T(8,128)(2,1)S(1)}, bf16[1,224,4096]{2,1,0:T(8,128)(2,1)}, u32[]{:S(2)}) copy-start(bf16[1,224,4096]{2,1,0:T(8,128)(2,1)} %fusion.6) | copy-start | bytes 5505028
  624.3 9.4 %all-to-all-start.2 = ((bf16[2,16,2]{1,2,0:T(2,128)(2,1)}), bf16[2,16,2]{1,2,0:T(2,128)(2,1)S(1)}, u32[]{:S(2)}, u32[]{:S(2)}) async-start(bf16[2,16,2]{1,2,0:T(2,128)(2,1)} %broadcast_in_dim.51), calls=%async_computation.3 | async-start | bytes 2048 | tf_op jit(solution)/shard_map/all_to_all | solution.py:30
  634.4 10.1 %all-to-all-start.1 = ((bf16[2,16,4096]{2,1,0:T(8,128)(2,1)}), bf16[2,16,4096]{2,1,0:T(8,128)(2,1)S(1)}, u32[]{:S(2)}, u32[]{:S(2)}) async-start(bf16[2,16,4096]{2,1,0:T(8,128)(2,1)} %broadcast_in_dim.50), calls=%async_computation.2 | async-start | bytes 524288 | tf_op jit(solution)/shard_map/all_to_all | solution.py:30
Sparse Core Ops, SparseCore 0:
  10.3 124.1 all-gather.2
  306.4 316.2 reduce-scatter.1
